TPU v7x, 32 devices: a whole 2x2x4 slice. The times are simulated.
32 devices in a mesh: row: 4 (over y, x), col: 8 (over z, core).
Axes of the slice: x: 2, y: 2, z: 4, core: 2. Of those that a mesh axis runs over, the one named last changes fastest.
Arguments:
- patches: bfloat16 [32, 128, 768], P('row', 'col'), may hold values from -6 to 6
- w_patch: bfloat16 [768, 6144], replicated, may hold values from -0.21875 to 0.21875
- patch_bias: bfloat16 [6144], replicated, may hold values from -5 to 5
- ln_gain: bfloat16 [6144], replicated, may hold values from 0.5 to 1.5
- w_qkv: bfloat16 [6144, 3, 48, 128], P(None, None, 'col'), may hold values from -1 to 1
- qk_gain: float32 [2, 48, 128], P(None, 'col'), may hold values from 0 to 6, as said below
- w_out: bfloat16 [48, 128, 6144], P('col', None, 'row'), may hold values from -0.078125 to 0.078125
Outputs:
- attn_branch: bfloat16 [4096, 6144], P(('row', 'col'))
Inputs may be any that keep to these rules, and one draw needn't show every extreme that they name: `qk_gain`: positive gains.
All inputs are finite; a program needn't handle non-finite values.
Results may differ from a plain program's by a relative error of at most 0.015.
Values may be sent and summed in bfloat16 or wider, within the bound.
A program may use at most 320 MiB of HBM per device.

v0:
```python
import math
import jax
import jax.numpy as jnp
from jax import lax
from jax.sharding import PartitionSpec as P

NORM_EPS = 1e-06


def sincos_table(row_ids, col_ids, model_width):
    quarter = model_width // 4
    frequency = 1.0 / 10000.0 ** (jnp.arange(quarter, dtype=jnp.float32) / quarter)
    row_angle = row_ids.astype(jnp.float32)[:, None] * frequency[None, :]
    col_angle = col_ids.astype(jnp.float32)[:, None] * frequency[None, :]
    return jnp.concatenate(
        [jnp.sin(row_angle), jnp.cos(row_angle), jnp.sin(col_angle), jnp.cos(col_angle)], axis=1
    )


def layer_norm(values, gain_row):
    mean_val = jnp.mean(values, axis=-1, keepdims=True)
    centered = values - mean_val
    variance = jnp.mean(centered * centered, axis=-1, keepdims=True)
    return centered * lax.rsqrt(variance + NORM_EPS) * gain_row


def local(patches, w_patch, patch_bias, ln_gain, w_qkv, qk_gain, w_out):
    tile_rows, tile_cols, pixel_width = patches.shape
    model_width = w_patch.shape[1]
    heads_here = w_qkv.shape[2]
    head_size = w_qkv.shape[3]
    col_count = lax.axis_size("col")
    block_tokens = tile_rows * tile_cols * col_count
    row_anchor = lax.axis_index("row") * tile_rows
    qkv_matrix = w_qkv.reshape(model_width, 3 * heads_here * head_size)
    bias_row = patch_bias.astype(jnp.float32)[None, :]
    gain_row = ln_gain.astype(jnp.float32)
    pixels = lax.all_gather(patches, "col", axis=1, tiled=True)
    piece_cols = pixels.shape[1]
    local_rows = jnp.repeat(jnp.arange(tile_rows, dtype=jnp.int32), piece_cols)
    local_cols = jnp.tile(jnp.arange(piece_cols, dtype=jnp.int32), tile_rows)
    flat_pixels = pixels.reshape(tile_rows * piece_cols, pixel_width)
    embedded = jnp.dot(flat_pixels, w_patch, preferred_element_type=jnp.float32) + bias_row
    embedded = embedded + sincos_table(row_anchor + local_rows, local_cols, model_width)
    normed = layer_norm(embedded, gain_row).astype(jnp.bfloat16)
    normed_piece = normed.reshape(tile_rows, piece_cols, model_width)
    project_piece_cols = normed_piece.shape[1]
    flat_normed = normed_piece.reshape(tile_rows * project_piece_cols, model_width)
    projected = jnp.dot(flat_normed, qkv_matrix, preferred_element_type=jnp.float32)
    projected = projected.reshape(tile_rows, project_piece_cols, 3 * heads_here * head_size)
    projected = projected.reshape(block_tokens, 3, heads_here, head_size)
    queries = layer_norm(projected[:, 0], qk_gain[0]).astype(jnp.bfloat16)
    keys_here = layer_norm(projected[:, 1], qk_gain[1]).astype(jnp.bfloat16)
    values_here = projected[:, 2].astype(jnp.bfloat16)
    query_heads = queries.transpose(1, 0, 2)
    scale_factor = 1.0 / math.sqrt(head_size)
    start_state = (
        jnp.full((heads_here, block_tokens), -1e30, jnp.float32),
        jnp.zeros((heads_here, block_tokens), jnp.float32),
        jnp.zeros((heads_here, block_tokens, head_size), jnp.float32),
    )
    key_piece = lax.all_gather(keys_here, "row", axis=0, tiled=True)
    value_piece = lax.all_gather(values_here, "row", axis=0, tiled=True)
    piece_len = key_piece.shape[0]
    key_block = math.gcd(piece_len, 1024)
    block_count = piece_len // key_block
    key_blocks = key_piece.reshape(block_count, key_block, heads_here, head_size)
    value_blocks = value_piece.reshape(block_count, key_block, heads_here, head_size)

    def step_block(state, block_args):
        run_peak, run_total, run_acc = state
        block_keys, block_values = block_args
        scores = (
            jnp.einsum("hqd,khd->hqk", query_heads, block_keys, preferred_element_type=jnp.float32)
            * scale_factor
        )
        new_peak = jnp.maximum(run_peak, jnp.max(scores, axis=2))
        rescale = jnp.exp(run_peak - new_peak)
        exponent = jnp.exp(scores - new_peak[:, :, None])
        new_total = run_total * rescale + jnp.sum(exponent, axis=2)
        weighted = jnp.einsum(
            "hqk,khd->hqd",
            exponent.astype(jnp.bfloat16),
            block_values,
            preferred_element_type=jnp.float32,
        )
        new_acc = run_acc * rescale[:, :, None] + weighted
        return ((new_peak, new_total, new_acc), None)

    final_state, unused = lax.scan(step_block, start_state, (key_blocks, value_blocks))
    peak_all, total_all, acc_all = final_state
    context = (acc_all / total_all[:, :, None]).astype(jnp.bfloat16)
    context = context.transpose(1, 0, 2).reshape(block_tokens, heads_here * head_size)
    out_weight = lax.all_gather(w_out, "row", axis=2, tiled=True).reshape(
        heads_here * head_size, model_width
    )
    return lax.psum_scatter(
        jnp.dot(context, out_weight, preferred_element_type=jnp.float32).astype(jnp.bfloat16),
        "col",
        scatter_dimension=0,
        tiled=True,
    )


def solution(mesh):
    return jax.shard_map(
        local,
        mesh=mesh,
        in_specs=(
            P("row", "col", None),
            P(),
            P(),
            P(),
            P(None, None, "col", None),
            P(None, "col", None),
            P("col", None, "row"),
        ),
        out_specs=P(("row", "col"), None),
        check_vma=False,
    )
```

profile of v0, /device:TPU:0, one launch (start us, length us, event | category | flops | bytes accessed | tf_op | source)
XLA Modules:
  0.0 631.0 jit_solution(16349719539641851866)
XLA Ops:
  6.5 0.0 all-gather.6.cloned.1.call-start
  6.5 0.7 all-gather.6.cloned.1.call-update
  7.3 0.0 all-gather.8.cloned.1.call-start
  7.3 0.7 convert_element_type.52
  8.0 0.0 copy-start.1
  8.0 0.0 copy-start.2
  8.0 36.8 %copy.13 = bf16[6144,3,6,128]{0,3,2,1:T(8,128)(2,1)} copy(bf16[6144,3,6,128]{3,0,2,1:T(8,128)(2,1)} %param.13) | data formatting | bytes 56623104 | tf_op args[4]
  44.8 0.0 copy-done.1
  44.8 0.0 copy-done.2
  44.9 46.9 %multiply_sine_fusion.1 = (f32[1024,1536]{1,0:T(8,128)}, f32[1024,1536]{1,0:T(8,128)}, f32[1024,1536]{1,0:T(8,128)}, f32[1024,1536]{1,0:T(8,128)}) fusion(f32[1536]{0:T(1024)S(1)} %negate_power_fusion, f32[1024]{0:T(1024)S(1)} %get-tuple-element.118, f32[1024]{0:T(1024)S(1)} %get-tuple-element.117), kind=kLoop, calls=%fused_computation.35 | loop fusion | flops 3145728 | bytes 25180160 | tf_op jit(solution)/shard_map/sin | solution.py:16
  91.8 0.0 all-gather.6.cloned.1.call-done
  91.8 24.2 %fusion.29 = (f32[1024]{0:T(1024)S(1)}, f32[1024,6144]{1,0:T(8,128)}) fusion(f32[1024,1536]{1,0:T(8,128)} %get-tuple-element.111, f32[1024,1536]{1,0:T(8,128)} %get-tuple-element.112, f32[1024,1536]{1,0:T(8,128)} %get-tuple-element.108, f32[1024,1536]{1,0:T(8,128)} %get-tuple-element.107, f32[6144]{0:T(1024)S(1)} %convert_element_type.52, ...), kind=kOutput, calls=%fused_computation.60 | convolution fusion | flops 9701424128 | bytes 61370368 | tf_op jit(solution)/shard_map/dot_general | solution.py:43
  116.1 10.2 %multiply_reduce_fusion = f32[1024]{0:T(1024)S(1)} fusion(f32[1024,6144]{1,0:T(8,128)} %get-tuple-element.116, f32[1024]{0:T(1024)S(1)} %broadcast_multiply_fusion.2), kind=kLoop, calls=%fused_computation.27 | loop fusion | flops 18873344 | bytes 25174016 | tf_op jit(solution)/shard_map/reduce_sum | solution.py:23
  126.2 36.4 %fusion.19 = f32[1024,3,6,128]{0,3,2,1:T(8,128)S(1)} fusion(bf16[6144,3,6,128]{0,3,2,1:T(8,128)(2,1)} %copy.13, f32[1024,6144]{1,0:T(8,128)} %get-tuple-element.116, f32[6144]{0:T(1024)S(1)} %convert_element_type.57, f32[1024]{0:T(1024)S(1)} %add_rsqrt_fusion.2, f32[1024]{0:T(1024)S(1)} %broadcast_multiply_fusion.2), kind=kOutput, calls=%fused_computation.22 | convolution fusion | flops 29016195072 | bytes 62947328 | tf_op jit(solution)/shard_map/dot_general | solution.py:49
  162.7 0.0 copy-start
  162.7 0.7 slice_reduce_fusion
  163.4 0.9 multiply_reduce_fusion.1
  164.4 1.9 copy-done
  166.3 1.8 fusion.26
  168.1 0.0 all-gather.8.cloned.1.call-update
  168.1 0.0 all-gather.12.cloned.1.call-start
  168.2 3.3 slice.33
  171.5 0.0 all-gather.12.cloned.1.call-update
  171.5 0.0 all-gather.10.cloned.1.call-start
  171.6 0.5 all-gather.10.cloned.1.call-update
  172.1 0.0 reduce-scatter.2.cloned.1.call-start
  172.2 1.1 copy.17
  173.3 67.7 %all-gather.8.cloned.1.call-done = bf16[4096,6,128]{0,2,1:T(8,128)(2,1)} async-done(((bf16[1024,6,128]{0,2,1:T(8,128)(2,1)}), bf16[4096,6,128]{0,2,1:T(8,128)(2,1)}) %all-gather.8.cloned.1.call-update) | async-done | bytes 6291472 | tf_op jit(solution)/shard_map/all_gather | solution.py:62
  241.0 11.3 %reshape.81 = bf16[4,1024,6,128]{1,0,3,2:T(4,128)(2,1)} reshape(bf16[4096,6,128]{0,2,1:T(8,128)(2,1)} %all-gather.8.cloned.1.call-done) | data formatting | bytes 12582912 | tf_op jit(solution)/shard_map/reshape | solution.py:67
  252.4 11.4 %copy.16 = bf16[4,1024,6,128]{3,1,2,0:T(8,128)(2,1)} copy(bf16[4,1024,6,128]{1,0,3,2:T(4,128)(2,1)} %reshape.81) | data formatting | bytes 12582912
  263.7 49.2 %all-gather.12.cloned.1.call-done = bf16[4096,1,6,128]{0,3,2,1:T(8,128)(2,1)} async-done(((bf16[1024,1,6,128]{0,3,2,1:T(8,128)(2,1)}), bf16[4096,1,6,128]{0,3,2,1:T(8,128)(2,1)}) %all-gather.12.cloned.1.call-update) | async-done | bytes 6291472 | tf_op jit(solution)/shard_map/all_gather | solution.py:63
  313.0 11.4 %reshape.82 = bf16[4,1024,6,128]{1,0,3,2:T(4,128)(2,1)} reshape(bf16[4096,1,6,128]{0,3,2,1:T(8,128)(2,1)} %all-gather.12.cloned.1.call-done) | data formatting | bytes 12582912 | tf_op jit(solution)/shard_map/reshape | solution.py:68
  324.4 11.3 %copy.18 = bf16[4,1024,6,128]{3,1,2,0:T(8,128)(2,1)} copy(bf16[4,1024,6,128]{1,0,3,2:T(4,128)(2,1)} %reshape.82) | data formatting | bytes 12582912
  335.7 143.7 %while.15 = (s32[]{:T(128)}, f32[6,1024]{1,0:T(8,128)S(1)}, f32[6,1024]{1,0:T(8,128)S(1)}, f32[6,1024,128]{2,1,0:T(8,128)}, bf16[4,1024,6,128]{3,1,2,0:T(8,128)(...) while((s32[]{:T(128)}, f32[6,1024]{1,0:T(8,128)S(1)}, ...), condition=%wide.region_9.10_spmd.clone, body=%wide.region_6.9_spmd.clone.sunk | while | flops 3273947136 | bytes 86901856 | solution.py:90
  335.7 11.5 %bitcast_reduce_fusion.2 = (f32[6,1024]{1,0:T(8,128)S(1)}, f32[6,1024,1024]{2,1,0:T(8,128)}) fusion(bf16[6,1024,128]{2,1,0:T(8,128)(2,1)S(1)} %get-tuple-element.195, bf16[4,1024,6,128]{3,1,2,0:T(8,128)(2,1)} %get-tuple-element.194, s32[]{:T(128)} %get-tuple-element.181), kind=kOutput, calls=%fused_computation.1.clone.1 | convolution fusion | flops 1623189504 | bytes 28336640 | tf_op jit(solution)/shard_map/while/body/eval_jaxpr/hqd,khd->hqk/dot_general | solution.py:74
  347.1 10.5 %fusion.43 = f32[6,1024]{1,0:T(8,128)S(1)} fusion(f32[6,1024,1024]{2,1,0:T(8,128)} %get-tuple-element.169, f32[6,1024]{1,0:T(8,128)S(1)} %select_maximum_fusion.2), kind=kLoop, calls=%fused_computation.4.clone.1 | loop fusion | flops 18868224 | bytes 25214976 | tf_op jit(solution)/shard_map/while/body/eval_jaxpr/reduce_sum | solution.py:80
  357.7 14.2 %fusion.45 = f32[6,1024,128]{2,1,0:T(8,128)} fusion(f32[6,1024,128]{2,1,0:T(8,128)} %get-tuple-element.184, f32[6,1024,1024]{2,1,0:T(8,128)} %get-tuple-element.169, f32[6,1024]{1,0:T(8,128)S(1)} %select_maximum_fusion.2, bf16[4,1024,6,128]{3,1,2,0:T(8,128)(2,1)} %get-tuple-element.196, s32[]{:T(128)} %get-tuple-element.181, ...), kind=kOutput, calls=%fused_computation.9.clone.1 | convolution fusion | flops 1631846400 | bytes 33079808 | tf_op jit(solution)/shard_map/while/body/eval_jaxpr/hqk,khd->hqd/dot_general | solution.py:81
  371.9 11.5 %bitcast_reduce_fusion.2 = (f32[6,1024]{1,0:T(8,128)S(1)}, f32[6,1024,1024]{2,1,0:T(8,128)}) fusion(bf16[6,1024,128]{2,1,0:T(8,128)(2,1)S(1)} %get-tuple-element.195, bf16[4,1024,6,128]{3,1,2,0:T(8,128)(2,1)} %get-tuple-element.194, s32[]{:T(128)} %get-tuple-element.181), kind=kOutput, calls=%fused_computation.1.clone.1 | convolution fusion | flops 1623189504 | bytes 28336640 | tf_op jit(solution)/shard_map/while/body/eval_jaxpr/hqd,khd->hqk/dot_general | solution.py:74
  383.4 10.5 %fusion.43 = f32[6,1024]{1,0:T(8,128)S(1)} fusion(f32[6,1024,1024]{2,1,0:T(8,128)} %get-tuple-element.169, f32[6,1024]{1,0:T(8,128)S(1)} %select_maximum_fusion.2), kind=kLoop, calls=%fused_computation.4.clone.1 | loop fusion | flops 18868224 | bytes 25214976 | tf_op jit(solution)/shard_map/while/body/eval_jaxpr/reduce_sum | solution.py:80
  394.0 13.7 %fusion.45 = f32[6,1024,128]{2,1,0:T(8,128)} fusion(f32[6,1024,128]{2,1,0:T(8,128)} %get-tuple-element.184, f32[6,1024,1024]{2,1,0:T(8,128)} %get-tuple-element.169, f32[6,1024]{1,0:T(8,128)S(1)} %select_maximum_fusion.2, bf16[4,1024,6,128]{3,1,2,0:T(8,128)(2,1)} %get-tuple-element.196, s32[]{:T(128)} %get-tuple-element.181, ...), kind=kOutput, calls=%fused_computation.9.clone.1 | convolution fusion | flops 1631846400 | bytes 33079808 | tf_op jit(solution)/shard_map/while/body/eval_jaxpr/hqk,khd->hqd/dot_general | solution.py:81
  407.8 11.5 %bitcast_reduce_fusion.2 = (f32[6,1024]{1,0:T(8,128)S(1)}, f32[6,1024,1024]{2,1,0:T(8,128)}) fusion(bf16[6,1024,128]{2,1,0:T(8,128)(2,1)S(1)} %get-tuple-element.195, bf16[4,1024,6,128]{3,1,2,0:T(8,128)(2,1)} %get-tuple-element.194, s32[]{:T(128)} %get-tuple-element.181), kind=kOutput, calls=%fused_computation.1.clone.1 | convolution fusion | flops 1623189504 | bytes 28336640 | tf_op jit(solution)/shard_map/while/body/eval_jaxpr/hqd,khd->hqk/dot_general | solution.py:74
  419.2 10.5 %fusion.43 = f32[6,1024]{1,0:T(8,128)S(1)} fusion(f32[6,1024,1024]{2,1,0:T(8,128)} %get-tuple-element.169, f32[6,1024]{1,0:T(8,128)S(1)} %select_maximum_fusion.2), kind=kLoop, calls=%fused_computation.4.clone.1 | loop fusion | flops 18868224 | bytes 25214976 | tf_op jit(solution)/shard_map/while/body/eval_jaxpr/reduce_sum | solution.py:80
  429.8 13.7 %fusion.45 = f32[6,1024,128]{2,1,0:T(8,128)} fusion(f32[6,1024,128]{2,1,0:T(8,128)} %get-tuple-element.184, f32[6,1024,1024]{2,1,0:T(8,128)} %get-tuple-element.169, f32[6,1024]{1,0:T(8,128)S(1)} %select_maximum_fusion.2, bf16[4,1024,6,128]{3,1,2,0:T(8,128)(2,1)} %get-tuple-element.196, s32[]{:T(128)} %get-tuple-element.181, ...), kind=kOutput, calls=%fused_computation.9.clone.1 | convolution fusion | flops 1631846400 | bytes 33079808 | tf_op jit(solution)/shard_map/while/body/eval_jaxpr/hqk,khd->hqd/dot_general | solution.py:81
  443.6 11.5 %bitcast_reduce_fusion.2 = (f32[6,1024]{1,0:T(8,128)S(1)}, f32[6,1024,1024]{2,1,0:T(8,128)}) fusion(bf16[6,1024,128]{2,1,0:T(8,128)(2,1)S(1)} %get-tuple-element.195, bf16[4,1024,6,128]{3,1,2,0:T(8,128)(2,1)} %get-tuple-element.194, s32[]{:T(128)} %get-tuple-element.181), kind=kOutput, calls=%fused_computation.1.clone.1 | convolution fusion | flops 1623189504 | bytes 28336640 | tf_op jit(solution)/shard_map/while/body/eval_jaxpr/hqd,khd->hqk/dot_general | solution.py:74
  455.1 10.5 %fusion.43 = f32[6,1024]{1,0:T(8,128)S(1)} fusion(f32[6,1024,1024]{2,1,0:T(8,128)} %get-tuple-element.169, f32[6,1024]{1,0:T(8,128)S(1)} %select_maximum_fusion.2), kind=kLoop, calls=%fused_computation.4.clone.1 | loop fusion | flops 18868224 | bytes 25214976 | tf_op jit(solution)/shard_map/while/body/eval_jaxpr/reduce_sum | solution.py:80
  465.6 13.7 %fusion.45 = f32[6,1024,128]{2,1,0:T(8,128)} fusion(f32[6,1024,128]{2,1,0:T(8,128)} %get-tuple-element.184, f32[6,1024,1024]{2,1,0:T(8,128)} %get-tuple-element.169, f32[6,1024]{1,0:T(8,128)S(1)} %select_maximum_fusion.2, bf16[4,1024,6,128]{3,1,2,0:T(8,128)(2,1)} %get-tuple-element.196, s32[]{:T(128)} %get-tuple-element.181, ...), kind=kOutput, calls=%fused_computation.9.clone.1 | convolution fusion | flops 1631846400 | bytes 33079808 | tf_op jit(solution)/shard_map/while/body/eval_jaxpr/hqk,khd->hqd/dot_general | solution.py:81
  479.4 0.0 all-gather.10.cloned.1.call-done
  479.4 15.5 %bitcast_convert_fusion = bf16[1024,6144]{1,0:T(8,128)(2,1)} fusion(bf16[6,128,6144]{2,1,0:T(8,128)(2,1)} %all-gather.10.cloned.1.call-done, f32[6,1024,128]{2,1,0:T(8,128)} %get-tuple-element.43, f32[6,1024]{1,0:T(8,128)S(1)} %get-tuple-element.44), kind=kOutput, calls=%fused_computation.25 | convolution fusion | flops 9671540736 | bytes 25190400 | tf_op jit(solution)/shard_map/dot_general | solution.py:98
  494.9 0.0 reduce-scatter.2.cloned.1.call-update
  494.9 129.6 %reduce-scatter.2.cloned.1.call-done = bf16[128,6144]{1,0:T(8,128)(2,1)} async-done(((bf16[1024,6144]{1,0:T(8,128)(2,1)}), bf16[128,6144]{1,0:T(8,128)(2,1)}) %reduce-scatter.2.cloned.1.call-update) | async-done | bytes 1572880 | tf_op jit(solution)/shard_map/reduce_scatter | solution.py:97
  (26 shorter events, 0.2 us)
Async XLA Ops:
  6.5 85.3 %all-gather.6.cloned.1.call-start = ((), (), s32[]{:S(2)}) async-start(), calls=%async_computation.1 | async-start | bytes 1769472 | tf_op jit(solution)/shard_map/all_gather | solution.py:38
  7.3 233.8 %all-gather.8.cloned.1.call-start = ((), (), s32[]{:S(2)}) async-start(), calls=%async_computation.2 | async-start | bytes 7864320 | tf_op jit(solution)/shard_map/all_gather | solution.py:62
  8.0 36.8 %copy-start.1 = (bf16[6144]{0:T(1024)(128)(2,1)S(1)}, bf16[6144]{0:T(1024)(128)(2,1)}, u32[]{:S(2)}) copy-start(bf16[6144]{0:T(1024)(128)(2,1)} %param.12) | copy-start | bytes 36868
  8.0 36.8 %copy-start.2 = (f32[2,6,128]{2,0,1:T(2,128)S(1)}, f32[2,6,128]{2,0,1:T(2,128)}, u32[]{:S(2)}) copy-start(f32[2,6,128]{2,0,1:T(2,128)} %param.14) | copy-start | bytes 18436
  162.7 3.6 copy-start
  168.1 144.8 %all-gather.12.cloned.1.call-start = ((), (), s32[]{:S(2)}) async-start(), calls=%async_computation.5 | async-start | bytes 7864320 | tf_op jit(solution)/shard_map/all_gather | solution.py:63
  171.5 307.9 %all-gather.10.cloned.1.call-start = ((), (), s32[]{:S(2)}) async-start(), calls=%async_computation.3 | async-start | bytes 11796480 | tf_op jit(solution)/shard_map/all_gather | solution.py:94
  172.1 452.4 %reduce-scatter.2.cloned.1.call-start = ((), (), s32[]{:S(2)}) async-start(), calls=%async_computation.4 | async-start | bytes 14155776 | tf_op jit(solution)/shard_map/reduce_scatter | solution.py:97
Sparse Core Ops, SparseCore 0:
  8.9 27.9 all-gather.5
  168.2 72.7 all-gather.7
  242.9 70.0 all-gather.11
  314.7 96.2 all-gather.9
  495.0 129.3 reduce-scatter.1
where the time goes:
time: 634 us; the launch traced here: 631 us
  waiting for transfers between devices  248 us (39%)
  matrix products  177 us (28%)
  other arithmetic  104 us (16%)
  local copies, waits for them, and re-layouts  88.6 us (14%)
  between operations  13.3 us (2%)
    reduce_scatter x1, waiting for transfers between devices, local(): lax.psum_scatter(jnp.dot(context, out_weight, preferred_element_type=jnp....  130 us
    all_gather x1, waiting for transfers between devices, local(): key_piece = lax.all_gather(keys_here, 'row', axis=0, tiled=True)  67.7 us
    unnamed x10, local copies, waits for them, and re-layouts  62.5 us
    dot_general x4, matrix products, step_block(): jnp.einsum('hqk,khd->hqd', exponent.astype(jnp.bfloat16), block_values, p...  55.5 us
    all_gather x1, waiting for transfers between devices, local(): value_piece = lax.all_gather(values_here, 'row', axis=0, tiled=True)  49.2 us
    sin x1, other arithmetic, sincos_table(): jnp.sin(row_angle)  46.9 us
    dot_general x4, matrix products, step_block(): jnp.einsum('hqd,khd->hqk', query_heads, block_keys, preferred_element_typ...  45.9 us
    reduce_sum x4, other arithmetic, step_block(): new_total = run_total * rescale + jnp.sum(exponent, axis=2)  42.2 us
  transfers between devices with their start and end apart: 5, of which 3 were waited for; matrix products, arithmetic and copies ran while one was open for 44% of the time, Pallas kernels for 0%

commit v1 on v0

--- a/solution.py
+++ b/solution.py
@@ -59,7 +59,12 @@
         jnp.zeros((heads_here, block_tokens), jnp.float32),
         jnp.zeros((heads_here, block_tokens, head_size), jnp.float32),
     )
-    key_piece = lax.all_gather(keys_here, "row", axis=0, tiled=True)
+    ring = [keys_here]
+    for hop in range(3):
+        ring.append(lax.ppermute(ring[-1], "row", [(dev, (dev + 1) % 4) for dev in range(4)]))
+    key_piece = jnp.roll(
+        jnp.concatenate(ring[::-1], axis=0), (lax.axis_index("row") + 1) * ring[0].shape[0], axis=0
+    )
     value_piece = lax.all_gather(values_here, "row", axis=0, tiled=True)
     piece_len = key_piece.shape[0]
     key_block = math.gcd(piece_len, 1024)

time: 634 us -> 698 us (1.10)
  waiting for transfers between devices: 248 us -> 307 us
    ppermute x0 -> x3, waiting for transfers between devices: none -> 177 us  [local(): lax.ppermute(ring[-1], 'row', [(dev, (dev + 1) % 4) for dev in range(4)])]
    all_gather x1 -> x0, waiting for transfers between devices: 67.7 us -> none  [local(): key_piece = lax.all_gather(keys_here, 'row', axis=0, tiled=True)]
    all_gather x1, waiting for transfers between devices: 49.2 us -> 0.01 us  [local(): value_piece = lax.all_gather(values_here, 'row', axis=0, tiled=True)]
    dynamic_slice x0 -> x2, local copies, waits for them, and re-layouts: none -> 11.9 us  [local(): jnp.roll(jnp.concatenate(ring[::-1], axis=0), (lax.axis_index('row') + 1)...]
    reshape x1 -> x0, local copies, waits for them, and re-layouts: 11.3 us -> none  [local(): key_piece.reshape(block_count, key_block, heads_here, head_size)]
    unnamed x10 -> x22, local copies, waits for them, and re-layouts: 62.5 us -> 61.3 us
  transfers between devices with their start and end apart: 5 -> 7, of which waited for: 3 -> 4; matrix products, arithmetic and copies ran while one was open for 44% -> 40% of each run, Pallas kernels for 0% -> 0%
where the time goes in v1:
time: 698 us; the launch traced here: 696 us
  waiting for transfers between devices  307 us (44%)
  matrix products  176 us (25%)
  other arithmetic  110 us (16%)
  local copies, waits for them, and re-layouts  85.9 us (12%)
  between operations  13.4 us (2%)
    ppermute x3, waiting for transfers between devices, local(): lax.ppermute(ring[-1], 'row', [(dev, (dev + 1) % 4) for dev in range(4)])  177 us
    reduce_scatter x1, waiting for transfers between devices, local(): lax.psum_scatter(jnp.dot(context, out_weight, preferred_element_type=jnp....  129 us
    unnamed x22, local copies, waits for them, and re-layouts  61.3 us
    dot_general x4, matrix products, step_block(): jnp.einsum('hqk,khd->hqd', exponent.astype(jnp.bfloat16), block_values, p...  53.8 us
    sin x1, other arithmetic, sincos_table(): jnp.sin(row_angle)  46.9 us
    dot_general x4, matrix products, step_block(): jnp.einsum('hqd,khd->hqk', query_heads, block_keys, preferred_element_typ...  46.4 us
    reduce_sum x4, other arithmetic, step_block(): new_total = run_total * rescale + jnp.sum(exponent, axis=2)  42.2 us
    dot_general x1, matrix products, local(): jnp.dot(flat_normed, qkv_matrix, preferred_element_type=jnp.float32)  36.4 us
  transfers between devices with their start and end apart: 7, of which 4 were waited for; matrix products, arithmetic and copies ran while one was open for 40% of the time, Pallas kernels for 0%

profile of v1, /device:TPU:0, one launch (start us, length us, event | category | flops | bytes accessed | tf_op | source)
XLA Modules:
  0.0 695.6 jit_solution(14699555758978112750)
XLA Ops:
  6.5 0.0 all-gather.5.cloned.1.call-start
  6.5 0.7 all-gather.5.cloned.1.call-update
  7.3 0.0 all-gather.9.cloned.1.call-start
  7.3 0.7 convert_element_type.52
  8.0 36.7 %copy.12 = bf16[6144,3,6,128]{0,3,2,1:T(8,128)(2,1)} copy(bf16[6144,3,6,128]{3,0,2,1:T(8,128)(2,1)} %param.13) | data formatting | bytes 56623104 | tf_op args[4]
  44.8 0.0 copy-done.4
  44.8 46.9 %multiply_sine_fusion.1 = (f32[1024,1536]{1,0:T(8,128)}, f32[1024,1536]{1,0:T(8,128)}, f32[1024,1536]{1,0:T(8,128)}, f32[1024,1536]{1,0:T(8,128)}) fusion(f32[1536]{0:T(1024)S(1)} %negate_power_fusion, f32[1024]{0:T(1024)S(1)} %get-tuple-element.118, f32[1024]{0:T(1024)S(1)} %get-tuple-element.117), kind=kLoop, calls=%fused_computation.35 | loop fusion | flops 3145728 | bytes 25180160 | tf_op jit(solution)/shard_map/sin | solution.py:16
  91.7 0.0 all-gather.5.cloned.1.call-done
  91.8 24.2 %fusion.29 = (f32[1024]{0:T(1024)S(1)}, f32[1024,6144]{1,0:T(8,128)}) fusion(f32[1024,1536]{1,0:T(8,128)} %get-tuple-element.111, f32[1024,1536]{1,0:T(8,128)} %get-tuple-element.112, f32[1024,1536]{1,0:T(8,128)} %get-tuple-element.108, f32[1024,1536]{1,0:T(8,128)} %get-tuple-element.107, f32[6144]{0:T(1024)S(1)} %convert_element_type.52, ...), kind=kOutput, calls=%fused_computation.69 | convolution fusion | flops 9701424128 | bytes 61370368 | tf_op jit(solution)/shard_map/dot_general | solution.py:43
  116.0 10.2 %multiply_reduce_fusion = f32[1024]{0:T(1024)S(1)} fusion(f32[1024,6144]{1,0:T(8,128)} %get-tuple-element.116, f32[1024]{0:T(1024)S(1)} %broadcast_multiply_fusion.2), kind=kLoop, calls=%fused_computation.27 | loop fusion | flops 18873344 | bytes 25174016 | tf_op jit(solution)/shard_map/reduce_sum | solution.py:23
  126.2 0.0 copy-start.5
  126.2 36.4 %fusion.19 = f32[1024,3,6,128]{0,3,2,1:T(8,128)S(1)} fusion(bf16[6144,3,6,128]{0,3,2,1:T(8,128)(2,1)} %copy.12, f32[1024,6144]{1,0:T(8,128)} %get-tuple-element.116, f32[6144]{0:T(1024)S(1)} %convert_element_type.57, f32[1024]{0:T(1024)S(1)} %add_rsqrt_fusion.2, f32[1024]{0:T(1024)S(1)} %broadcast_multiply_fusion.2), kind=kOutput, calls=%fused_computation.22 | convolution fusion | flops 29016195072 | bytes 62947328 | tf_op jit(solution)/shard_map/dot_general | solution.py:49
  162.6 0.0 copy-start
  162.6 3.6 copy-done
  166.2 1.5 slice.33
  167.6 0.0 all-gather.9.cloned.1.call-update
  167.7 0.0 all-gather.7.cloned.1.call-start
  167.7 0.0 copy-done.5
  167.7 0.0 copy-start.1
  167.8 3.7 slice_reduce_fusion
  171.5 4.3 multiply_reduce_fusion.1
  175.8 0.0 copy-done.1
  175.9 1.9 fusion.26
  177.8 3.0 collective-permute-start
  180.8 61.9 %collective-permute-done = bf16[1024,6,128]{0,2,1:T(8,128)(2,1)S(1)} collective-permute-done((bf16[1024,6,128]{0,2,1:T(8,128)(2,1)S(1)}, bf16[1024,6,128]{0,2,1:T(8,128)(2,1)S(1)}, u32[]{:S(2)}, u32[]{:S(2)}) %collective-permute-start) | collective-permute-done | bytes 1572896 | tf_op jit(solution)/shard_map/ppermute | solution.py:64
  242.7 1.1 copy-done.2
  243.8 0.0 collective-permute-start.1
  243.8 56.7 %collective-permute-done.1 = bf16[1024,6,128]{0,2,1:T(8,128)(2,1)} collective-permute-done((bf16[1024,6,128]{0,2,1:T(8,128)(2,1)S(1)}, bf16[1024,6,128]{0,2,1:T(8,128)(2,1)}, u32[]{:S(2)}, u32[]{:S(2)}) %collective-permute-start.1) | collective-permute-done | bytes 1572896 | tf_op jit(solution)/shard_map/ppermute | solution.py:64
  300.5 0.0 collective-permute-start.2
  300.5 0.0 all-gather.7.cloned.1.call-update
  300.5 0.0 reduce-scatter.2.cloned.1.call-start
  300.6 2.1 copy.17
  302.8 0.0 copy-start.3
  302.8 58.4 %collective-permute-done.2 = bf16[1024,6,128]{0,2,1:T(8,128)(2,1)} collective-permute-done((bf16[1024,6,128]{0,2,1:T(8,128)(2,1)}, bf16[1024,6,128]{0,2,1:T(8,128)(2,1)}, u32[]{:S(2)}, u32[]{:S(2)}) %collective-permute-start.2) | collective-permute-done | bytes 1572896 | tf_op jit(solution)/shard_map/ppermute | solution.py:64
  361.2 1.5 constant_dynamic-update-slice_fusion.7
  362.7 1.5 constant_dynamic-update-slice_fusion.6
  364.3 0.0 copy-done.3
  364.3 0.1 constant_dynamic-update-slice_fusion.5
  364.4 0.1 constant_dynamic-update-slice_fusion.4
  364.6 1.5 constant_dynamic-update-slice_fusion.3
  366.1 1.5 constant_dynamic-update-slice_fusion.2
  367.6 0.1 constant_dynamic-update-slice_fusion.1
  367.8 0.1 constant_dynamic-update-slice_fusion
  367.9 3.3 constant_dynamic-slice_fusion
  371.2 8.6 %copy.14 = bf16[4096,6,128]{2,0,1:T(8,128)(2,1)} copy(bf16[4096,6,128]{0,2,1:T(8,128)(2,1)} %constant_dynamic-slice_fusion) | data formatting | bytes 12582912 | tf_op jit(solution)/shard_map/jit(_roll_dynamic)/dynamic_slice | solution.py:65
  379.8 11.1 %reshape.82 = bf16[4,1024,6,128]{1,0,3,2:T(4,128)(2,1)} reshape(bf16[4096,1,6,128]{0,3,2,1:T(8,128)(2,1)} %all-gather.9.cloned.1.call-done) | data formatting | bytes 12582912 | tf_op jit(solution)/shard_map/reshape | solution.py:73
  390.9 11.2 %copy.18 = bf16[4,1024,6,128]{3,1,2,0:T(8,128)(2,1)} copy(bf16[4,1024,6,128]{1,0,3,2:T(4,128)(2,1)} %reshape.82) | data formatting | bytes 12582912
  402.1 142.5 %while.15 = (s32[]{:T(128)}, f32[6,1024]{1,0:T(8,128)S(1)}, f32[6,1024]{1,0:T(8,128)S(1)}, f32[6,1024,128]{2,1,0:T(8,128)}, bf16[4,1024,6,128]{3,1,0,2:T(8,128)(...) while((s32[]{:T(128)}, f32[6,1024]{1,0:T(8,128)S(1)}, ...), condition=%wide.region_9.10_spmd.clone, body=%wide.region_6.9_spmd.clone.sunk | while | flops 3273947136 | bytes 86901856 | solution.py:95
  402.1 11.6 %bitcast_reduce_fusion.2 = (f32[6,1024]{1,0:T(8,128)S(1)}, f32[6,1024,1024]{2,1,0:T(8,128)}) fusion(bf16[6,1024,128]{2,1,0:T(8,128)(2,1)S(1)} %get-tuple-element.195, bf16[4,1024,6,128]{3,1,0,2:T(8,128)(2,1)} %get-tuple-element.194, s32[]{:T(128)} %get-tuple-element.181), kind=kOutput, calls=%fused_computation.1.clone.1 | convolution fusion | flops 1623189504 | bytes 28336640 | tf_op jit(solution)/shard_map/while/body/eval_jaxpr/hqd,khd->hqk/dot_general | solution.py:79
  413.7 10.5 %fusion.43 = f32[6,1024]{1,0:T(8,128)S(1)} fusion(f32[6,1024,1024]{2,1,0:T(8,128)} %get-tuple-element.169, f32[6,1024]{1,0:T(8,128)S(1)} %select_maximum_fusion.2), kind=kLoop, calls=%fused_computation.4.clone.1 | loop fusion | flops 18868224 | bytes 25214976 | tf_op jit(solution)/shard_map/while/body/eval_jaxpr/reduce_sum | solution.py:85
  424.3 12.8 %fusion.45 = f32[6,1024,128]{2,1,0:T(8,128)} fusion(f32[6,1024,128]{2,1,0:T(8,128)} %get-tuple-element.184, f32[6,1024,1024]{2,1,0:T(8,128)} %get-tuple-element.169, f32[6,1024]{1,0:T(8,128)S(1)} %select_maximum_fusion.2, bf16[4,1024,6,128]{3,1,2,0:T(8,128)(2,1)} %get-tuple-element.196, s32[]{:T(128)} %get-tuple-element.181, ...), kind=kOutput, calls=%fused_computation.9.clone.1 | convolution fusion | flops 1631846400 | bytes 33079808 | tf_op jit(solution)/shard_map/while/body/eval_jaxpr/hqk,khd->hqd/dot_general | solution.py:86
  437.1 11.6 %bitcast_reduce_fusion.2 = (f32[6,1024]{1,0:T(8,128)S(1)}, f32[6,1024,1024]{2,1,0:T(8,128)}) fusion(bf16[6,1024,128]{2,1,0:T(8,128)(2,1)S(1)} %get-tuple-element.195, bf16[4,1024,6,128]{3,1,0,2:T(8,128)(2,1)} %get-tuple-element.194, s32[]{:T(128)} %get-tuple-element.181), kind=kOutput, calls=%fused_computation.1.clone.1 | convolution fusion | flops 1623189504 | bytes 28336640 | tf_op jit(solution)/shard_map/while/body/eval_jaxpr/hqd,khd->hqk/dot_general | solution.py:79
  448.7 10.5 %fusion.43 = f32[6,1024]{1,0:T(8,128)S(1)} fusion(f32[6,1024,1024]{2,1,0:T(8,128)} %get-tuple-element.169, f32[6,1024]{1,0:T(8,128)S(1)} %select_maximum_fusion.2), kind=kLoop, calls=%fused_computation.4.clone.1 | loop fusion | flops 18868224 | bytes 25214976 | tf_op jit(solution)/shard_map/while/body/eval_jaxpr/reduce_sum | solution.py:85
  459.3 13.7 %fusion.45 = f32[6,1024,128]{2,1,0:T(8,128)} fusion(f32[6,1024,128]{2,1,0:T(8,128)} %get-tuple-element.184, f32[6,1024,1024]{2,1,0:T(8,128)} %get-tuple-element.169, f32[6,1024]{1,0:T(8,128)S(1)} %select_maximum_fusion.2, bf16[4,1024,6,128]{3,1,2,0:T(8,128)(2,1)} %get-tuple-element.196, s32[]{:T(128)} %get-tuple-element.181, ...), kind=kOutput, calls=%fused_computation.9.clone.1 | convolution fusion | flops 1631846400 | bytes 33079808 | tf_op jit(solution)/shard_map/while/body/eval_jaxpr/hqk,khd->hqd/dot_general | solution.py:86
  472.9 11.6 %bitcast_reduce_fusion.2 = (f32[6,1024]{1,0:T(8,128)S(1)}, f32[6,1024,1024]{2,1,0:T(8,128)}) fusion(bf16[6,1024,128]{2,1,0:T(8,128)(2,1)S(1)} %get-tuple-element.195, bf16[4,1024,6,128]{3,1,0,2:T(8,128)(2,1)} %get-tuple-element.194, s32[]{:T(128)} %get-tuple-element.181), kind=kOutput, calls=%fused_computation.1.clone.1 | convolution fusion | flops 1623189504 | bytes 28336640 | tf_op jit(solution)/shard_map/while/body/eval_jaxpr/hqd,khd->hqk/dot_general | solution.py:79
  484.5 10.5 %fusion.43 = f32[6,1024]{1,0:T(8,128)S(1)} fusion(f32[6,1024,1024]{2,1,0:T(8,128)} %get-tuple-element.169, f32[6,1024]{1,0:T(8,128)S(1)} %select_maximum_fusion.2), kind=kLoop, calls=%fused_computation.4.clone.1 | loop fusion | flops 18868224 | bytes 25214976 | tf_op jit(solution)/shard_map/while/body/eval_jaxpr/reduce_sum | solution.py:85
  495.1 13.7 %fusion.45 = f32[6,1024,128]{2,1,0:T(8,128)} fusion(f32[6,1024,128]{2,1,0:T(8,128)} %get-tuple-element.184, f32[6,1024,1024]{2,1,0:T(8,128)} %get-tuple-element.169, f32[6,1024]{1,0:T(8,128)S(1)} %select_maximum_fusion.2, bf16[4,1024,6,128]{3,1,2,0:T(8,128)(2,1)} %get-tuple-element.196, s32[]{:T(128)} %get-tuple-element.181, ...), kind=kOutput, calls=%fused_computation.9.clone.1 | convolution fusion | flops 1631846400 | bytes 33079808 | tf_op jit(solution)/shard_map/while/body/eval_jaxpr/hqk,khd->hqd/dot_general | solution.py:86
  508.8 11.6 %bitcast_reduce_fusion.2 = (f32[6,1024]{1,0:T(8,128)S(1)}, f32[6,1024,1024]{2,1,0:T(8,128)}) fusion(bf16[6,1024,128]{2,1,0:T(8,128)(2,1)S(1)} %get-tuple-element.195, bf16[4,1024,6,128]{3,1,0,2:T(8,128)(2,1)} %get-tuple-element.194, s32[]{:T(128)} %get-tuple-element.181), kind=kOutput, calls=%fused_computation.1.clone.1 | convolution fusion | flops 1623189504 | bytes 28336640 | tf_op jit(solution)/shard_map/while/body/eval_jaxpr/hqd,khd->hqk/dot_general | solution.py:79
  520.4 10.5 %fusion.43 = f32[6,1024]{1,0:T(8,128)S(1)} fusion(f32[6,1024,1024]{2,1,0:T(8,128)} %get-tuple-element.169, f32[6,1024]{1,0:T(8,128)S(1)} %select_maximum_fusion.2), kind=kLoop, calls=%fused_computation.4.clone.1 | loop fusion | flops 18868224 | bytes 25214976 | tf_op jit(solution)/shard_map/while/body/eval_jaxpr/reduce_sum | solution.py:85
  531.0 13.7 %fusion.45 = f32[6,1024,128]{2,1,0:T(8,128)} fusion(f32[6,1024,128]{2,1,0:T(8,128)} %get-tuple-element.184, f32[6,1024,1024]{2,1,0:T(8,128)} %get-tuple-element.169, f32[6,1024]{1,0:T(8,128)S(1)} %select_maximum_fusion.2, bf16[4,1024,6,128]{3,1,2,0:T(8,128)(2,1)} %get-tuple-element.196, s32[]{:T(128)} %get-tuple-element.181, ...), kind=kOutput, calls=%fused_computation.9.clone.1 | convolution fusion | flops 1631846400 | bytes 33079808 | tf_op jit(solution)/shard_map/while/body/eval_jaxpr/hqk,khd->hqd/dot_general | solution.py:86
  544.6 0.0 all-gather.7.cloned.1.call-done
  544.6 15.3 %bitcast_convert_fusion = bf16[1024,6144]{1,0:T(8,128)(2,1)} fusion(bf16[6,128,6144]{2,1,0:T(8,128)(2,1)} %all-gather.7.cloned.1.call-done, f32[6,1024,128]{2,1,0:T(8,128)} %get-tuple-element.43, f32[6,1024]{1,0:T(8,128)S(1)} %get-tuple-element.44), kind=kOutput, calls=%fused_computation.25 | convolution fusion | flops 9671540736 | bytes 25190400 | tf_op jit(solution)/shard_map/dot_general | solution.py:103
  560.0 0.0 reduce-scatter.2.cloned.1.call-update
  560.0 129.1 %reduce-scatter.2.cloned.1.call-done = bf16[128,6144]{1,0:T(8,128)(2,1)} async-done(((bf16[1024,6144]{1,0:T(8,128)(2,1)}), bf16[128,6144]{1,0:T(8,128)(2,1)}) %reduce-scatter.2.cloned.1.call-update) | async-done | bytes 1572880 | tf_op jit(solution)/shard_map/reduce_scatter | solution.py:102
  (29 shorter events, 0.2 us)
Async XLA Ops:
  6.5 85.2 %all-gather.5.cloned.1.call-start = ((), (), s32[]{:S(2)}) async-start(), calls=%async_computation.1 | async-start | bytes 1769472 | tf_op jit(solution)/shard_map/all_gather | solution.py:38
  7.3 372.6 %all-gather.9.cloned.1.call-start = ((), (), s32[]{:S(2)}) async-start(), calls=%async_computation.4 | async-start | bytes 7864320 | tf_op jit(solution)/shard_map/all_gather | solution.py:68
  8.0 36.7 %copy-start.4 = (bf16[6144]{0:T(1024)(128)(2,1)S(1)}, bf16[6144]{0:T(1024)(128)(2,1)}, u32[]{:S(2)}) copy-start(bf16[6144]{0:T(1024)(128)(2,1)} %param.12) | copy-start | bytes 36868
  126.2 41.6 %copy-start.5 = (f32[2,6,128]{2,0,1:T(2,128)S(1)}, f32[2,6,128]{2,0,1:T(2,128)}, u32[]{:S(2)}) copy-start(f32[2,6,128]{2,0,1:T(2,128)} %param.14) | copy-start | bytes 18436
  162.6 3.6 copy-start
  167.7 377.0 %all-gather.7.cloned.1.call-start = ((), (), s32[]{:S(2)}) async-start(), calls=%async_computation.2 | async-start | bytes 11796480 | tf_op jit(solution)/shard_map/all_gather | solution.py:99
  167.7 8.1 %copy-start.1 = (f32[1024,3,6,128]{0,3,2,1:T(8,128)S(1)}, f32[1024,3,6,128]{0,3,2,1:T(8,128)}, u32[]{:S(2)}) copy-start(f32[1024,3,6,128]{0,3,2,1:T(8,128)} %copy-done) | copy-start | bytes 28311556
  177.8 64.9 %collective-permute-start = (bf16[1024,6,128]{0,2,1:T(8,128)(2,1)S(1)}, bf16[1024,6,128]{0,2,1:T(8,128)(2,1)S(1)}, u32[]{:S(2)}, u32[]{:S(2)}) collective-permute-start(bf16[1024,6,128]{0,2,1:T(8,128)(2,1)S(1)} %get-tuple-element.106), channel_id=1, source_target_pairs={{0,8},{8,16},{16,24},{24,0},{1,9},{9,17},{17,25},{25,1},{2,10},{10... | collective-permute-start | bytes 4718600 | tf_op jit(solution)/shard_map/ppermute | solution.py:64
  242.7 1.1 copy-start.2
  243.8 56.7 %collective-permute-start.1 = (bf16[1024,6,128]{0,2,1:T(8,128)(2,1)S(1)}, bf16[1024,6,128]{0,2,1:T(8,128)(2,1)}, u32[]{:S(2)}, u32[]{:S(2)}) collective-permute-start(bf16[1024,6,128]{0,2,1:T(8,128)(2,1)S(1)} %collective-permute-done), channel_id=1, source_target_pairs={{0,8},{8,16},{16,24},{24,0},{1,9},{9,17},{17,25},{25,1},{2,10},{10... | collective-permute-start | bytes 4718600 | tf_op jit(solution)/shard_map/ppermute | solution.py:64
  300.5 60.7 %collective-permute-start.2 = (bf16[1024,6,128]{0,2,1:T(8,128)(2,1)}, bf16[1024,6,128]{0,2,1:T(8,128)(2,1)}, u32[]{:S(2)}, u32[]{:S(2)}) collective-permute-start(bf16[1024,6,128]{0,2,1:T(8,128)(2,1)} %collective-permute-done.1), channel_id=1, source_target_pairs={{0,8},{8,16},{16,24},{24,0},{1,9},{9,17},{17,25},{25,1},{2,10},{10... | collective-permute-start | bytes 4718600 | tf_op jit(solution)/shard_map/ppermute | solution.py:64
  300.5 388.6 %reduce-scatter.2.cloned.1.call-start = ((), (), s32[]{:S(2)}) async-start(), calls=%async_computation.3 | async-start | bytes 14155776 | tf_op jit(solution)/shard_map/reduce_scatter | solution.py:102
  302.8 61.5 %copy-start.3 = (bf16[1024,6,128]{0,2,1:T(8,128)(2,1)S(1)}, bf16[1024,6,128]{0,2,1:T(8,128)(2,1)}, u32[]{:S(2)}) copy-start(bf16[1024,6,128]{0,2,1:T(8,128)(2,1)} %copy-done.2) | copy-start | bytes 4718596
Sparse Core Ops, SparseCore 0:
  8.9 27.9 all-gather.4
  167.8 118.7 all-gather.8
  300.7 119.6 all-gather.6
  560.1 128.9 reduce-scatter.1
